TPU v7x, 32 devices: a whole 2x2x4 slice. The times are simulated.
32 devices in a mesh: table: 16 (over z, y, x), dp: 2 (over core).
Axes of the slice: x: 2, y: 2, z: 4, core: 2. Of those that a mesh axis runs over, the one named last changes fastest.
Arguments:
- tables: bfloat16 [4, 65536, 128], P(None, 'table'), may hold values from -6 to 6
- owner_ids: int32 [32, 4, 256, 1], P(('table', 'dp')), may hold values from 0 to 15; in each aligned block of 256 rows (0 to 255, 256 to 511, ..., all dimensions but the last counted through in order) at most 32 rows name the same one
- row_ids: int32 [32, 4, 256], P(('table', 'dp')), may hold values from 0 to 4095
- session_of: int32 [32, 256], P(('table', 'dp')), may hold values from 0 to 1, never falling along the last dimension, each value on 1 to 200 neighbouring positions
- relevance: float32 [32, 256], P(('table', 'dp')), may hold values from 0.1 to 10
- logit_bias: float32 [32, 256], P(('table', 'dp')), may hold values from -400 to 400
- w_hidden: float32 [512, 512], replicated, may hold values from -0.25 to 0.25
- bias_hidden: float32 [512], replicated, may hold values from -3 to 3
- w_score: float32 [512], replicated, may hold values from -0.9 to 0.9
Outputs:
- emb_step: float32 [4, 65536, 128], P(None, ('table', 'dp'))
- step_hidden: float32 [512, 512], replicated
- step_bias: float32 [512], replicated
- step_score: float32 [512], replicated
- loss: float32 [], replicated
Inputs may be any that keep to these rules, and one draw needn't show every extreme that they name: `owner_ids`: among one device's impressions, for one table, at most 32 name the same owner. `session_of`: session numbers never fall along a device's impressions; each of a device's 2 sessions has 1 to 200 impressions.
All inputs are finite; a program needn't handle non-finite values.
Results may differ from a plain program's by a relative error of at most 0.001.
The roundings to bfloat16 on the way count: a program that leaves them out, or rounds other values in their place, can miss the bound.
Values may be sent and summed in bfloat16 or wider, within the bound.
A program may use at most 64 MiB of HBM per device.

v0:
```python
import jax
import jax.numpy as jnp
from jax import lax
from jax.sharding import PartitionSpec as P

SESS_DEV = 2


def silu_slope(pre_val):
    logistic = jax.nn.sigmoid(pre_val)
    return logistic * (1.0 + pre_val * (1.0 - logistic))


def session_terms(scores, session_ids, relevance, sessions):
    member = session_ids[None, :] == jnp.arange(sessions, dtype=jnp.int32)[:, None]
    highest = jnp.max(jnp.where(member, scores[None, :], -jnp.inf), axis=1)
    highest_each = jnp.sum(jnp.where(member, highest[:, None], 0.0), axis=0)
    shifted = scores - highest_each
    exponent = jnp.exp(shifted)
    totals = jnp.sum(jnp.where(member, exponent[None, :], 0.0), axis=1)
    weights = jnp.sum(jnp.where(member, relevance[None, :], 0.0), axis=1)
    total_each = jnp.sum(jnp.where(member, totals[:, None], 0.0), axis=0)
    weight_each = jnp.sum(jnp.where(member, weights[:, None], 0.0), axis=0)
    probability = exponent / total_each
    target = relevance / weight_each
    loss_sum = jnp.sum(jnp.log(totals)) - jnp.sum(target * shifted)
    return (loss_sum, probability - target)


def selector(indices, count):
    return (indices[:, None] == jnp.arange(count, dtype=jnp.int32)[None, :]).astype(jnp.bfloat16)


def pick_rows(indices, source):
    return jnp.dot(
        selector(indices, source.shape[0]), source, preferred_element_type=jnp.float32
    ).astype(jnp.bfloat16)


def place_rows(indices, values, count):
    return lax.dot_general(
        selector(indices, count),
        values,
        (((0,), (0,)), ((), ())),
        preferred_element_type=jnp.float32,
    )


def on_device(
    tables, owner_ids, row_ids, session_of, relevance, logit_bias, w_hidden, bias_hidden, w_score
):
    owners = lax.axis_size("table")
    devices = owners * lax.axis_size("dp")
    table_count, shard_rows, emb_width = tables.shape
    owner_now = owner_ids[0, :, :, 0]
    rows_now = row_ids[0]
    imp_count = owner_now.shape[1]
    capacity = 2 * imp_count // owners
    slot_total = owners * capacity
    one_hot = (owner_now[:, :, None] == jnp.arange(owners, dtype=jnp.int32)).astype(jnp.float32)
    places = jnp.arange(imp_count, dtype=jnp.int32)
    lower_tri = (places[:, None] >= places[None, :]).astype(jnp.float32)
    running = jnp.einsum("ij,tjo->tio", lower_tri, one_hot, precision=lax.Precision.HIGHEST)
    rank_in = (jnp.sum(running * one_hot, axis=2) - 1.0).astype(jnp.int32)
    slot_of = owner_now * capacity + rank_in
    slot_hot = (slot_of[:, :, None] == jnp.arange(slot_total, dtype=jnp.int32)).astype(jnp.int32)
    wanted = jnp.sum(slot_hot * rows_now[:, :, None], axis=1) + shard_rows * (
        1 - jnp.sum(slot_hot, axis=1)
    )
    requested = lax.all_to_all(
        wanted.reshape(table_count, owners, capacity),
        "table",
        split_axis=1,
        concat_axis=1,
        tiled=True,
    )
    served = lax.map(
        lambda pair: pick_rows(pair[0], pair[1]),
        (requested.reshape(table_count, slot_total), tables),
    )
    served = served.reshape(table_count, owners, capacity, emb_width)
    hidden_bf = w_hidden.astype(jnp.bfloat16)
    returned = lax.all_to_all(served, "table", split_axis=1, concat_axis=1, tiled=True).reshape(
        table_count, slot_total, emb_width
    )
    gathered = lax.map(lambda pair: pick_rows(pair[0], pair[1]), (slot_of, returned))
    inputs = jnp.transpose(gathered, (1, 0, 2)).reshape(imp_count, table_count * emb_width)
    pre_act = jnp.dot(inputs, hidden_bf, preferred_element_type=jnp.float32)
    pre_act = pre_act + bias_hidden
    hidden = jax.nn.silu(pre_act)
    scores = jnp.dot(hidden, w_score, precision=lax.Precision.HIGHEST) + logit_bias[0]
    loss_sum, score_grad = session_terms(scores, session_of[0], relevance[0], SESS_DEV)
    pre_grad = score_grad[:, None] * w_score[None, :] * silu_slope(pre_act)
    pre_grad_bf = pre_grad.astype(jnp.bfloat16)
    weight_grad = lax.dot_general(
        inputs, pre_grad_bf, (((0,), (0,)), ((), ())), preferred_element_type=jnp.float32
    )
    bias_grad = jnp.sum(pre_grad, axis=0)
    score_weight_grad = jnp.dot(score_grad, hidden, precision=lax.Precision.HIGHEST)
    input_grad = jnp.dot(pre_grad_bf, hidden_bf.T, preferred_element_type=jnp.float32).astype(
        jnp.bfloat16
    )
    input_grad = jnp.transpose(input_grad.reshape(imp_count, table_count, emb_width), (1, 0, 2))
    outgoing = lax.map(
        lambda pair: place_rows(pair[0], pair[1], slot_total).astype(jnp.bfloat16),
        (slot_of, input_grad),
    )
    incoming = lax.all_to_all(
        outgoing.reshape(table_count, owners, capacity, emb_width),
        "table",
        split_axis=1,
        concat_axis=1,
        tiled=True,
    )
    summed = lax.map(
        lambda pair: place_rows(pair[0], pair[1], shard_rows),
        (
            requested.reshape(table_count, slot_total),
            incoming.reshape(table_count, slot_total, emb_width),
        ),
    )
    own_rows = lax.psum_scatter(summed, "dp", scatter_dimension=1, tiled=True)
    emb_step = own_rows / (jnp.sqrt(jnp.mean(own_rows * own_rows, axis=2, keepdims=True)) + 1e-06)
    param_count = w_hidden.size + bias_hidden.size + w_score.size
    weight_tot, bias_tot, score_tot, loss_tot = lax.psum(
        (weight_grad, bias_grad, score_weight_grad, loss_sum), ("table", "dp")
    )
    mean_sq = (
        jnp.sum(weight_tot * weight_tot)
        + jnp.sum(bias_tot * bias_tot)
        + jnp.sum(score_tot * score_tot)
    ) / param_count
    factor = 1.0 / jnp.sqrt(mean_sq + 1e-06)
    step_hidden = weight_tot * factor
    loss = loss_tot / (SESS_DEV * devices)
    return (emb_step, step_hidden, bias_tot * factor, score_tot * factor, loss)


def solution(mesh):
    in_specs = (
        P(None, "table", None),
        P(("table", "dp"), None, None, None),
        P(("table", "dp"), None, None),
        P(("table", "dp"), None),
        P(("table", "dp"), None),
        P(("table", "dp"), None),
        P(),
        P(),
        P(),
    )
    out_specs = (P(None, ("table", "dp"), None), P(), P(), P(), P())
    return jax.shard_map(
        on_device, mesh=mesh, in_specs=in_specs, out_specs=out_specs, check_vma=False
    )
```

profile of v0, /device:TPU:0, one launch (start us, length us, event | category | flops | bytes accessed | tf_op | source)
XLA Modules:
  0.0 230.8 jit_solution(7807377824483772021)
XLA Ops:
  8.0 0.7 copy.45
  8.9 0.7 convert_add_fusion
  9.6 1.2 convert_reduce_fusion
  10.9 0.7 reshape.88
  11.6 8.3 %all-to-all-start = ((s32[16,1,128]{2,1,0:T(1,128)}), s32[16,1,128]{2,1,0:T(1,128)S(1)}, u32[]{:S(2)}, u32[]{:S(2)}) async-start(s32[16,1,128]{2,1,0:T(1,128)} %reshape.88), calls=%async_computation | async-start | bytes 16384 | tf_op jit(solution)/shard_map/all_to_all | solution.py:70
  20.0 7.2 %all-to-all-done = s32[16,1,128]{2,1,0:T(1,128)S(1)} async-done(((s32[16,1,128]{2,1,0:T(1,128)}), s32[16,1,128]{2,1,0:T(1,128)S(1)}, u32[]{:S(2)}, u32[]{:S(2)}) %all-to-all-start) | async-done | bytes 8224 | tf_op jit(solution)/shard_map/all_to_all | solution.py:70
  27.7 0.7 reduce
  28.7 11.4 %while.40 = (s32[]{:T(128)}, bf16[4,512,128]{2,1,0:T(8,128)(2,1)S(1)}, s32[4,512]{1,0:T(4,128)S(1)}, bf16[4,4096,128]{2,1,0:T(8,128)(2,1)}, s32[]{:T(128)}) while((s32[]{:T(128)}, bf16[4,512,128]{2,1,0:T(8,128)(2,1)S(1)}, s32[4,512]{1,0:T(4,128)S(1)}, bf16[4,4096,128]{2,1,0:T(8,128)(2,1)}, s32[]{:T(128)}) %tuple.66), condition=%wide.region_4.5_spmd, body=%wide.region_3.4_spmd.sunk | while | flops 539033600 | bytes 1186889 | solution.py:77
  28.7 2.8 %fusion.58 = bf16[4,512,128]{2,1,0:T(8,128)(2,1)S(1)} fusion(bf16[4,512,128]{2,1,0:T(8,128)(2,1)S(1)} %get-tuple-element.248, s32[]{:T(128)S(6)} %copy.55, s32[512]{0:T(512)S(1)} %bitcast.108, bf16[4,4096,128]{2,1,0:T(8,128)(2,1)} %get-tuple-element.255), kind=kOutput, calls=%fused_computation.5.clone.1 | convolution fusion | flops 539033600 | bytes 1182720 | tf_op jit(solution)/shard_map/while/body/eval_jaxpr/dot_general | solution.py:35
  31.5 2.8 %fusion.58 = bf16[4,512,128]{2,1,0:T(8,128)(2,1)S(1)} fusion(bf16[4,512,128]{2,1,0:T(8,128)(2,1)S(1)} %get-tuple-element.248, s32[]{:T(128)S(6)} %copy.55, s32[512]{0:T(512)S(1)} %bitcast.108, bf16[4,4096,128]{2,1,0:T(8,128)(2,1)} %get-tuple-element.255), kind=kOutput, calls=%fused_computation.5.clone.1 | convolution fusion | flops 539033600 | bytes 1182720 | tf_op jit(solution)/shard_map/while/body/eval_jaxpr/dot_general | solution.py:35
  34.4 2.8 %fusion.58 = bf16[4,512,128]{2,1,0:T(8,128)(2,1)S(1)} fusion(bf16[4,512,128]{2,1,0:T(8,128)(2,1)S(1)} %get-tuple-element.248, s32[]{:T(128)S(6)} %copy.55, s32[512]{0:T(512)S(1)} %bitcast.108, bf16[4,4096,128]{2,1,0:T(8,128)(2,1)} %get-tuple-element.255), kind=kOutput, calls=%fused_computation.5.clone.1 | convolution fusion | flops 539033600 | bytes 1182720 | tf_op jit(solution)/shard_map/while/body/eval_jaxpr/dot_general | solution.py:35
  37.2 2.8 %fusion.58 = bf16[4,512,128]{2,1,0:T(8,128)(2,1)S(1)} fusion(bf16[4,512,128]{2,1,0:T(8,128)(2,1)S(1)} %get-tuple-element.248, s32[]{:T(128)S(6)} %copy.55, s32[512]{0:T(512)S(1)} %bitcast.108, bf16[4,4096,128]{2,1,0:T(8,128)(2,1)} %get-tuple-element.255), kind=kOutput, calls=%fused_computation.5.clone.1 | convolution fusion | flops 539033600 | bytes 1182720 | tf_op jit(solution)/shard_map/while/body/eval_jaxpr/dot_general | solution.py:35
  40.1 0.9 copy.29
  40.9 3.6 %all-to-all-start.1 = ((bf16[4,16,32,128]{3,2,0,1:T(8,128)(2,1)}), bf16[4,16,32,128]{3,2,0,1:T(8,128)(2,1)S(1)}, u32[]{:S(2)}, u32[]{:S(2)}) async-start(bf16[4,16,32,128]{3,2,0,1:T(8,128)(2,1)} %copy.29), calls=%async_computation.1 | async-start | bytes 1048576 | tf_op jit(solution)/shard_map/all_to_all | solution.py:83
  44.5 13.9 %all-to-all-done.1 = bf16[4,16,32,128]{3,2,0,1:T(8,128)(2,1)S(1)} async-done(((bf16[4,16,32,128]{3,2,0,1:T(8,128)(2,1)}), bf16[4,16,32,128]{3,2,0,1:T(8,128)(2,1)S(1)}, u32[]{:S(2)}, u32[]{:S(2)}) %all-to-all-start.1) | async-done | bytes 524320 | tf_op jit(solution)/shard_map/all_to_all | solution.py:83
  58.5 1.8 while.41
  63.0 1.9 while.42
  64.8 0.9 copy.33
  65.7 3.8 %all-to-all-start.2 = ((bf16[4,16,32,128]{3,2,0,1:T(8,128)(2,1)}), bf16[4,16,32,128]{3,2,0,1:T(8,128)(2,1)S(1)}, u32[]{:S(2)}, u32[]{:S(2)}) async-start(bf16[4,16,32,128]{3,2,0,1:T(8,128)(2,1)} %copy.33), calls=%async_computation.2 | async-start | bytes 1048576 | tf_op jit(solution)/shard_map/all_to_all | solution.py:108
  69.5 1.4 fusion.34
  71.1 12.4 %all-to-all-done.2 = bf16[4,16,32,128]{3,2,0,1:T(8,128)(2,1)S(1)} async-done(((bf16[4,16,32,128]{3,2,0,1:T(8,128)(2,1)}), bf16[4,16,32,128]{3,2,0,1:T(8,128)(2,1)S(1)}, u32[]{:S(2)}, u32[]{:S(2)}) %all-to-all-start.2) | async-done | bytes 524320 | tf_op jit(solution)/shard_map/all_to_all | solution.py:108
  83.5 15.1 %while.43 = (s32[]{:T(128)}, f32[4,4096,128]{2,1,0:T(8,128)}, s32[4,512]{1,0:T(4,128)S(1)}, bf16[4,512,128]{2,1,0:T(8,128)(2,1)S(1)}, s32[]{:T(128)}) while((s32[]{:T(128)}, f32[4,4096,128]{2,1,0:T(8,128)}, s32[4,512]{1,0:T(4,128)S(1)}, bf16[4,512,128]{2,1,0:T(8,128)(2,1)S(1)}, s32[]{:T(128)}) %tuple.85), condition=%wide.region_16.17_spmd, body=%wide.region_15.16_spmd.sunk | while | flops 538968064 | bytes 2235465 | solution.py:115
  83.6 3.8 %fusion.64 = f32[4,4096,128]{2,1,0:T(8,128)} fusion(f32[4,4096,128]{2,1,0:T(8,128)} %get-tuple-element.293, s32[]{:T(128)S(6)} %copy.73, s32[512]{0:T(512)S(1)} %bitcast.109, bf16[4,512,128]{2,1,0:T(8,128)(2,1)S(1)} %get-tuple-element.300), kind=kOutput, calls=%fused_computation.31.clone.1 | convolution fusion | flops 538968064 | bytes 2231296 | tf_op jit(solution)/shard_map/while/body/eval_jaxpr/dot_general | solution.py:41
  87.4 3.7 %fusion.64 = f32[4,4096,128]{2,1,0:T(8,128)} fusion(f32[4,4096,128]{2,1,0:T(8,128)} %get-tuple-element.293, s32[]{:T(128)S(6)} %copy.73, s32[512]{0:T(512)S(1)} %bitcast.109, bf16[4,512,128]{2,1,0:T(8,128)(2,1)S(1)} %get-tuple-element.300), kind=kOutput, calls=%fused_computation.31.clone.1 | convolution fusion | flops 538968064 | bytes 2231296 | tf_op jit(solution)/shard_map/while/body/eval_jaxpr/dot_general | solution.py:41
  91.1 3.8 %fusion.64 = f32[4,4096,128]{2,1,0:T(8,128)} fusion(f32[4,4096,128]{2,1,0:T(8,128)} %get-tuple-element.293, s32[]{:T(128)S(6)} %copy.73, s32[512]{0:T(512)S(1)} %bitcast.109, bf16[4,512,128]{2,1,0:T(8,128)(2,1)S(1)} %get-tuple-element.300), kind=kOutput, calls=%fused_computation.31.clone.1 | convolution fusion | flops 538968064 | bytes 2231296 | tf_op jit(solution)/shard_map/while/body/eval_jaxpr/dot_general | solution.py:41
  94.9 3.8 %fusion.64 = f32[4,4096,128]{2,1,0:T(8,128)} fusion(f32[4,4096,128]{2,1,0:T(8,128)} %get-tuple-element.293, s32[]{:T(128)S(6)} %copy.73, s32[512]{0:T(512)S(1)} %bitcast.109, bf16[4,512,128]{2,1,0:T(8,128)(2,1)S(1)} %get-tuple-element.300), kind=kOutput, calls=%fused_computation.31.clone.1 | convolution fusion | flops 538968064 | bytes 2231296 | tf_op jit(solution)/shard_map/while/body/eval_jaxpr/dot_general | solution.py:41
  101.3 39.0 %all-reduce = (f32[512]{0:T(512)S(1)}, f32[512]{0:T(512)S(1)}, f32[]{:T(128)}) all-reduce(f32[512]{0:T(512)S(1)} %fusion.44, f32[512]{0:T(512)S(1)} %bitcast.122, f32[]{:T(128)S(6)} %sub.30), channel_id=1, replica_groups=mesh['table'=16,'dp'=2] {'table','dp'}, use_global_device_ids=true, to_apply=%region_22.23 | all-reduce | flops 1025 | bytes 8200 | tf_op jit(solution)/shard_map/psum | solution.py:125
  141.6 66.5 %all-reduce.3.cloned.1.call-done = f32[512,512]{1,0:T(8,128)} async-done(((f32[512,512]{1,0:T(8,128)}), f32[512,512]{1,0:T(8,128)}) %all-reduce.3.cloned.1.call-update) | async-done | bytes 1048592 | tf_op jit(solution)/shard_map/psum | solution.py:125
  208.1 2.1 multiply_reduce_fusion.1
  213.3 2.3 broadcast_multiply_fusion
  215.6 3.5 %multiply_reduce_fusion = f32[4,2048]{1,0:T(4,128)S(1)} fusion(f32[4,2048,128]{2,1,0:T(8,128)} %reduce-scatter.2.cloned.1.call-done), kind=kLoop, calls=%fused_computation.37 | loop fusion | flops 2088960 | bytes 4227072 | tf_op jit(solution)/shard_map/reduce_sum | solution.py:123
  219.2 3.1 %broadcast_divide_fusion = f32[4,2048,128]{2,1,0:T(8,128)} fusion(f32[4,2048,128]{2,1,0:T(8,128)S(1)} %copy-done, f32[4,2048]{1,0:T(4,128)S(1)} %sqrt_add_fusion), kind=kLoop, calls=%fused_computation.38 | loop fusion | flops 1048576 | bytes 8421376 | tf_op jit(solution)/shard_map/div | solution.py:123
  (84 shorter events, 10.4 us)
Async XLA Ops:
  11.6 15.6 %all-to-all-start = ((s32[16,1,128]{2,1,0:T(1,128)}), s32[16,1,128]{2,1,0:T(1,128)S(1)}, u32[]{:S(2)}, u32[]{:S(2)}) async-start(s32[16,1,128]{2,1,0:T(1,128)} %reshape.88), calls=%async_computation | async-start | bytes 16384 | tf_op jit(solution)/shard_map/all_to_all | solution.py:70
  40.0 20.3 %copy-start.1 = (f32[512,512]{1,0:T(8,128)S(1)}, f32[512,512]{1,0:T(8,128)}, u32[]{:S(2)}) copy-start(f32[512,512]{1,0:T(8,128)} %param.23) | copy-start | bytes 3145732
  40.0 20.3 %copy-start.5 = (f32[512]{0:T(512)S(1)}, f32[512]{0:T(512)}, u32[]{:S(2)}) copy-start(f32[512]{0:T(512)} %param.24) | copy-start | bytes 6148
  40.0 20.6 %copy-start.4 = (f32[512]{0:T(512)S(1)}, f32[512]{0:T(512)}, u32[]{:S(2)}) copy-start(f32[512]{0:T(512)} %param.25) | copy-start | bytes 6148
  40.9 17.6 %all-to-all-start.1 = ((bf16[4,16,32,128]{3,2,0,1:T(8,128)(2,1)}), bf16[4,16,32,128]{3,2,0,1:T(8,128)(2,1)S(1)}, u32[]{:S(2)}, u32[]{:S(2)}) async-start(bf16[4,16,32,128]{3,2,0,1:T(8,128)(2,1)} %copy.29), calls=%async_computation.1 | async-start | bytes 1048576 | tf_op jit(solution)/shard_map/all_to_all | solution.py:83
  44.5 16.8 %copy-start.6 = (f32[1,256]{1,0:T(1,128)S(1)}, f32[1,256]{1,0:T(1,128)}, u32[]{:S(2)}) copy-start(f32[1,256]{1,0:T(1,128)} %param.22) | copy-start | bytes 3076
  44.5 16.8 %copy-start.2 = (s32[1,256]{1,0:T(1,128)S(1)}, s32[1,256]{1,0:T(1,128)}, u32[]{:S(2)}) copy-start(s32[1,256]{1,0:T(1,128)} %param.20) | copy-start | bytes 3076
  44.5 17.0 %copy-start.3 = (f32[1,256]{1,0:T(1,128)S(1)}, f32[1,256]{1,0:T(1,128)}, u32[]{:S(2)}) copy-start(f32[1,256]{1,0:T(1,128)} %param.21) | copy-start | bytes 3076
  65.7 17.8 %all-to-all-start.2 = ((bf16[4,16,32,128]{3,2,0,1:T(8,128)(2,1)}), bf16[4,16,32,128]{3,2,0,1:T(8,128)(2,1)S(1)}, u32[]{:S(2)}, u32[]{:S(2)}) async-start(bf16[4,16,32,128]{3,2,0,1:T(8,128)(2,1)} %copy.33), calls=%async_computation.2 | async-start | bytes 1048576 | tf_op jit(solution)/shard_map/all_to_all | solution.py:108
  69.5 138.6 %all-reduce.3.cloned.1.call-start = ((), (), s32[]{:S(2)}) async-start(), calls=%async_computation.5 | async-start | bytes 2097152 | tf_op jit(solution)/shard_map/psum | solution.py:125
  71.0 144.6 %reduce-scatter.2.cloned.1.call-start = ((), (), s32[]{:S(2)}) async-start(), calls=%async_computation.4 | async-start | bytes 12582912 | tf_op jit(solution)/shard_map/reduce_scatter | solution.py:122
  215.6 3.5 %copy-start = (f32[4,2048,128]{2,1,0:T(8,128)S(1)}, f32[4,2048,128]{2,1,0:T(8,128)}, u32[]{:S(2)}) copy-start(f32[4,2048,128]{2,1,0:T(8,128)} %reduce-scatter.2.cloned.1.call-done) | copy-start | bytes 12582916
Sparse Core Ops, SparseCore 0:
  76.1 131.9 all-reduce.2
Sparse Core Ops, SparseCore 1:
  98.8 14.4 reduce-scatter.1
where the time goes:
time: 232 us; the launch traced here: 231 us
  waiting for transfers between devices  100 us (43%)
  blocking collectives  39 us (17%)
  matrix products  32.6 us (14%)
  between operations  20.8 us (9%)
  other arithmetic  17.3 us (7%)
  starting transfers between devices  15.8 us (7%)
  local copies, waits for them, and re-layouts  4.78 us (2%)
    psum x1, waiting for transfers between devices, on_device(): lax.psum((weight_grad, bias_grad, score_weight_grad, loss_sum), ('table',...  66.5 us
    psum x1, blocking collectives, on_device(): lax.psum((weight_grad, bias_grad, score_weight_grad, loss_sum), ('table',...  39 us
    dot_general x8, matrix products, place_rows(): lax.dot_general(selector(indices, count), values, (((0,), (0,)), ((), ())...  16.8 us
    all_to_all x1, waiting for transfers between devices, on_device(): lax.all_to_all(served, 'table', split_axis=1, concat_axis=1, tiled=True)  13.9 us
    all_to_all x1, waiting for transfers between devices, on_device(): lax.all_to_all(outgoing.reshape(table_count, owners, capacity, emb_width)...  12.4 us
    dot_general x8, matrix products, pick_rows(): jnp.dot(selector(indices, source.shape[0]), source, preferred_element_typ...  12.4 us
    all_to_all x1, starting transfers between devices, on_device(): lax.all_to_all(wanted.reshape(table_count, owners, capacity), 'table', sp...  8.34 us
    all_to_all x1, waiting for transfers between devices, on_device(): lax.all_to_all(wanted.reshape(table_count, owners, capacity), 'table', sp...  7.23 us
  transfers between devices with their start and end apart: 5, of which 4 were waited for; matrix products, arithmetic and copies ran while one was open for 10% of the time, Pallas kernels for 0%

commit v1 on v0

--- a/solution.py
+++ b/solution.py
@@ -1,6 +1,9 @@
 import jax
 import jax.numpy as jnp
 from jax import lax
+from jax.experimental import pallas as pl
+from jax.experimental.pallas import tpu as pltpu
+import functools
 from jax.sharding import PartitionSpec as P
 
 SESS_DEV = 2
@@ -105,6 +108,16 @@
         lambda pair: place_rows(pair[0], pair[1], slot_total).astype(jnp.bfloat16),
         (slot_of, input_grad),
     )
+    if capacity % 16 == 0 and w_hidden.shape[0] == w_hidden.shape[1]:
+        return finish_kernel(
+            outgoing.reshape(table_count, owners, capacity, emb_width),
+            requested.reshape(table_count, slot_total),
+            weight_grad,
+            bias_grad,
+            score_weight_grad,
+            loss_sum,
+            shard_rows,
+        )
     incoming = lax.all_to_all(
         outgoing.reshape(table_count, owners, capacity, emb_width),
         "table",
@@ -134,6 +147,250 @@
     step_hidden = weight_tot * factor
     loss = loss_tot / (SESS_DEV * devices)
     return (emb_step, step_hidden, bias_tot * factor, score_tot * factor, loss)
+
+
+MESH = pl.DeviceIdType.MESH
+
+
+def finish_body(
+    sizes, out_ref, ids_ref, dense_ref, emb_ref, step_ref, small_ref,
+    grads, swapped, ids_other, emb_rows, from_other, from_plane, from_column, sum_pair, sum_plane,
+    total, grad_send, grad_recv, own_sem, swap_send, swap_recv, ids_sems, pair_sems, plane_send,
+    plane_recv, column_send, column_recv, emb_sem,
+):
+    tables, owners, capacity, width, half_rows, inner, outer, hid, sessions = sizes
+    slots = owners * capacity
+    me = lax.axis_index("table")
+    core = lax.axis_index("dp")
+    low, high = lax.rem(me, inner), me // inner
+    other = (me, 1 - core)
+
+    barrier = pltpu.get_barrier_semaphore()
+
+    def greet(step, carry):
+        pl.semaphore_signal(
+            barrier, inc=1, device_id=(lax.rem(me + step, owners), core), device_id_type=MESH
+        )
+        return carry
+
+    pl.semaphore_signal(barrier, inc=1, device_id=other, device_id_type=MESH)
+    lax.fori_loop(1, owners, greet, 0)
+    pl.semaphore_wait(barrier, owners)
+
+    def remote(src, dst, send, recv, to):
+        return pltpu.make_async_remote_copy(
+            src_ref=src, dst_ref=dst, send_sem=send, recv_sem=recv, device_id=to,
+            device_id_type=MESH,
+        )
+
+    pair_up = remote(dense_ref.at[1 - core], from_other, pair_sems.at[0], pair_sems.at[1], other)
+    pair_up.start()
+    ids_copy = remote(ids_ref, ids_other, ids_sems.at[0], ids_sems.at[1], other)
+    ids_copy.start()
+
+    def own_copy(table):
+        return pltpu.make_async_copy(
+            out_ref.at[table, me], grads.at[table, me], own_sem.at[table]
+        )
+
+    def send_grads(table):
+        own_copy(table).start()
+
+        def send_one(step, carry):
+            owner = lax.rem(me + step, owners)
+            remote(
+                out_ref.at[table, owner], grads.at[table, me], grad_send.at[table],
+                grad_recv.at[table], (owner, core),
+            ).start()
+            return carry
+
+        lax.fori_loop(1, owners, send_one, 0)
+
+    def all_grads(table):
+        return remote(
+            out_ref.at[table, pl.ds(0, owners - 1)], grads.at[table, pl.ds(0, owners - 1)],
+            grad_send.at[table], grad_recv.at[table], other,
+        )
+
+    def swap(table):
+        return remote(
+            grads.at[table], swapped.at[table], swap_send.at[table], swap_recv.at[table], other
+        )
+
+    def arrive(table):
+        own_copy(table).wait()
+        all_grads(table).wait()
+        swap(table).start()
+
+    block = 256
+
+    def emb_copy(table):
+        return pltpu.make_async_copy(emb_rows.at[table], emb_ref.at[table], emb_sem.at[table])
+
+    def place(table):
+        swap(table).wait()
+        ids_mine = ids_ref[pl.ds(table, 1), :]
+        ids_theirs = ids_other[pl.ds(table, 1), :]
+        rows_mine = grads[table].reshape(slots, width)
+        rows_theirs = swapped[table].reshape(slots, width)
+
+        def place_block(step, carry):
+            at = lax.broadcasted_iota(jnp.int32, (block, slots), 0) + (
+                core * half_rows + step * block
+            )
+            hot_mine = jnp.where(at == ids_mine, 1.0, 0.0).astype(jnp.bfloat16)
+            hot_theirs = jnp.where(at == ids_theirs, 1.0, 0.0).astype(jnp.bfloat16)
+            summed = jnp.dot(hot_mine, rows_mine, preferred_element_type=jnp.float32)
+            summed = summed + jnp.dot(hot_theirs, rows_theirs, preferred_element_type=jnp.float32)
+            mean = jnp.sum(summed * summed, axis=1, keepdims=True) / width
+            emb_rows[table, pl.ds(pl.multiple_of(step * block, block), block), :] = summed / (
+                jnp.sqrt(mean) + 1e-06
+            )
+            return carry
+
+        lax.fori_loop(0, half_rows // block, place_block, 0)
+        emb_copy(table).start()
+
+    def plane_copies(phase, src_of, dst_of):
+        return [
+            remote(
+                src_of(lax.rem(low + step, inner)), dst_of(step - 1), plane_send.at[phase, step - 1],
+                plane_recv.at[phase, step - 1], (high * inner + lax.rem(low + step, inner), core),
+            )
+            for step in range(1, inner)
+        ]
+
+    def column_copies(phase, src_of, dst_of):
+        return [
+            remote(
+                src_of(lax.rem(high + step, outer)), dst_of(step - 1), column_send.at[phase, step - 1],
+                column_recv.at[phase, step - 1], (lax.rem(high + step, outer) * inner + low, core),
+            )
+            for step in range(1, outer)
+        ]
+
+    def run(copies):
+        for copy in copies:
+            copy.start()
+
+    def finish(copies):
+        for copy in copies:
+            copy.wait()
+
+    send_grads(0)
+    pair_up.wait()
+    sum_pair[...] = dense_ref[core] + from_other[...]
+    plane_sum = plane_copies(0, lambda to: sum_pair.at[to], lambda slot: from_plane.at[slot])
+    run(plane_sum)
+    for table in range(1, tables):
+        send_grads(table)
+    ids_copy.wait()
+    finish(plane_sum)
+    part = sum_pair[low]
+    for slot in range(inner - 1):
+        part = part + from_plane[slot]
+    sum_plane[...] = part
+    column_sum = column_copies(0, lambda to: sum_plane.at[to], lambda slot: from_column.at[slot])
+    run(column_sum)
+    arrive(0)
+    finish(column_sum)
+    part = sum_plane[high]
+    for slot in range(outer - 1):
+        part = part + from_column[slot]
+    total[core, low, high] = part
+    column_share = column_copies(
+        1, lambda to: total.at[core, low, high], lambda slot: total.at[core, low, high]
+    )
+    run(column_share)
+    place(0)
+    for table in range(1, tables):
+        if table == 1:
+            finish(column_share)
+            plane_share = plane_copies(
+                1, lambda to: total.at[core, low], lambda slot: total.at[core, low]
+            )
+            run(plane_share)
+        arrive(table)
+        if table == tables - 1:
+            finish(plane_share)
+            pair_down = remote(
+                total.at[core], total.at[core], pair_sems.at[2], pair_sems.at[3], other
+            )
+            pair_down.start()
+        place(table)
+    pair_down.wait()
+    every = total[...].reshape(2 * owners * dense_ref.shape[3], dense_ref.shape[4])
+    weights, extra = every[:, :hid], every[:, hid:]
+    counted = lax.broadcasted_iota(jnp.int32, extra.shape, 1) < 2
+    counts = jnp.where(counted, extra, 0.0)
+    squares = jnp.sum(weights * weights, keepdims=True) + jnp.sum(counts * counts, keepdims=True)
+    factor = 1.0 / jnp.sqrt(squares / (hid * hid + 2 * hid) + 1e-06)
+    step_ref[...] = weights * factor
+    scaled = jnp.where(counted, extra * factor, extra / sessions)
+    small_ref[...] = scaled.T
+    for table in range(tables):
+        emb_copy(table).wait()
+
+
+def finish_kernel(outgoing, requested, weight_grad, bias_grad, score_grad, loss_sum, shard_rows):
+    tables, owners, capacity, width = outgoing.shape
+    hid = weight_grad.shape[0]
+    half_rows = shard_rows // 2
+    inner = 1
+    while inner * inner < owners:
+        inner *= 2
+    outer = owners // inner
+    rows = hid // (2 * owners)
+    lane = jnp.arange(128, dtype=jnp.int32)[None, :]
+    extra = jnp.where(
+        lane == 0,
+        bias_grad[:, None],
+        jnp.where(
+            lane == 1,
+            score_grad[:, None],
+            jnp.where(
+                (lane == 2) & (jnp.arange(hid, dtype=jnp.int32)[:, None] == 0), loss_sum, 0.0
+            ),
+        ),
+    )
+    dense = jnp.concatenate([weight_grad, extra], axis=1)
+    wide = dense.shape[1]
+    dense = dense.reshape(2, inner, outer, rows, wide)
+    sizes = (
+        tables, owners, capacity, width, half_rows, inner, outer, hid,
+        SESS_DEV * owners * 2,
+    )
+    f32, bf16 = jnp.float32, jnp.bfloat16
+    dma = pltpu.SemaphoreType.DMA
+    vmem = pl.BlockSpec(memory_space=pltpu.VMEM)
+    emb_step, step_hidden, small = pl.pallas_call(
+        functools.partial(finish_body, sizes),
+        out_shape=(
+            jax.ShapeDtypeStruct((tables, half_rows, width), f32),
+            jax.ShapeDtypeStruct((hid, hid), f32),
+            jax.ShapeDtypeStruct((128, hid), f32),
+        ),
+        in_specs=[vmem] * 3,
+        out_specs=(pl.BlockSpec(memory_space=pl.ANY), vmem, vmem),
+        scratch_shapes=[
+            pltpu.VMEM((tables, owners, capacity, width), bf16),
+            pltpu.VMEM((tables, owners, capacity, width), bf16),
+            pltpu.VMEM(requested.shape, jnp.int32),
+            pltpu.VMEM((tables, half_rows, width), f32),
+            pltpu.VMEM((inner, outer, rows, wide), f32),
+            pltpu.VMEM((inner - 1, outer, rows, wide), f32),
+            pltpu.VMEM((outer - 1, rows, wide), f32),
+            pltpu.VMEM((inner, outer, rows, wide), f32),
+            pltpu.VMEM((outer, rows, wide), f32),
+            pltpu.VMEM((2, inner, outer, rows, wide), f32),
+            dma((tables,)), dma((tables,)), dma((tables,)), dma((tables,)), dma((tables,)),
+            dma((2,)), dma((4,)),
+            dma((2, inner - 1)), dma((2, inner - 1)), dma((2, outer - 1)), dma((2, outer - 1)),
+            dma((tables,)),
+        ],
+        compiler_params=pltpu.CompilerParams(collective_id=1, has_side_effects=True),
+    )(outgoing, requested, dense)
+    return (emb_step, step_hidden, small[0], small[1], small[2, 0])
 
 
 def solution(mesh):

time: 232 us -> 114 us (0.49)
  waiting for transfers between devices: 100 us -> 21.1 us
  Pallas kernels: 0 us -> 43 us
  blocking collectives: 39 us -> 0 us
  between operations: 20.8 us -> 2.21 us
  matrix products: 32.6 us -> 16.5 us
  other arithmetic: 17.3 us -> 4.77 us
  local copies, waits for them, and re-layouts: 4.78 us -> 13.4 us
  starting transfers between devices: 15.8 us -> 11.9 us
    psum x1 -> x0, waiting for transfers between devices: 66.5 us -> none  [on_device(): lax.psum((weight_grad, bias_grad, score_weight_grad, loss_sum), ('table',...]
    pallas_call x0 -> x1, Pallas kernels: none -> 43 us  [finish_kernel(): pl.pallas_call(functools.partial(finish_body, sizes), out_shape=(jax.Shap...]
    psum x1 -> x0, blocking collectives: 39 us -> none  [on_device(): lax.psum((weight_grad, bias_grad, score_weight_grad, loss_sum), ('table',...]
    dot_general x8 -> x4, matrix products: 16.8 us -> 1.71 us  [place_rows(): lax.dot_general(selector(indices, count), values, (((0,), (0,)), ((), ())...]
    all_to_all x1 -> x0, waiting for transfers between devices: 12.4 us -> none  [on_device(): lax.all_to_all(outgoing.reshape(table_count, owners, capacity, emb_width)...]
    reduce_sum x3 -> x0, other arithmetic: 6.2 us -> none  [the longest x1 3.5 us: on_device(): jnp.mean(own_rows * own_rows, axis=2, keepdims=True)]
    unnamed x17 -> x19, local copies, waits for them, and re-layouts: 1.51 us -> 7.04 us
    all_to_all x1 -> x0, starting transfers between devices: 3.81 us -> none  [on_device(): lax.all_to_all(outgoing.reshape(table_count, owners, capacity, emb_width)...]
  transfers between devices with their start and end apart: 5 -> 2, of which waited for: 4 -> 2; matrix products, arithmetic and copies ran while one was open for 10% -> 0% of each run, Pallas kernels for 0% -> 0%
where the time goes in v1:
time: 114 us; the launch traced here: 113 us
  Pallas kernels  43 us (38%)
  waiting for transfers between devices  21.1 us (19%)
  matrix products  16.5 us (14%)
  local copies, waits for them, and re-layouts  13.4 us (12%)
  starting transfers between devices  11.9 us (10%)
  other arithmetic  4.77 us (4%)
  between operations  2.21 us (2%)
    pallas_call x1, Pallas kernels, finish_kernel(): pl.pallas_call(functools.partial(finish_body, sizes), out_shape=(jax.Shap...  43 us
    all_to_all x1, waiting for transfers between devices, on_device(): lax.all_to_all(served, 'table', split_axis=1, concat_axis=1, tiled=True)  13.9 us
    dot_general x8, matrix products, pick_rows(): jnp.dot(selector(indices, source.shape[0]), source, preferred_element_typ...  12.3 us
    all_to_all x1, starting transfers between devices, on_device(): lax.all_to_all(wanted.reshape(table_count, owners, capacity), 'table', sp...  8.34 us
    all_to_all x1, waiting for transfers between devices, on_device(): lax.all_to_all(wanted.reshape(table_count, owners, capacity), 'table', sp...  7.23 us
    unnamed x19, local copies, waits for them, and re-layouts  7.04 us
    all_to_all x1, starting transfers between devices, on_device(): lax.all_to_all(served, 'table', split_axis=1, concat_axis=1, tiled=True)  3.57 us
    slice x2, local copies, waits for them, and re-layouts, finish_kernel(): return (emb_step, step_hidden, small[0], small[1], small[2, 0])  2.57 us
  transfers between devices with their start and end apart: 2, of which 2 were waited for; matrix products, arithmetic and copies ran while one was open for 0% of the time, Pallas kernels for 0%

profile of v1, /device:TPU:0, one launch (start us, length us, event | category | flops | bytes accessed | tf_op | source)
XLA Modules:
  0.0 113.3 jit_solution(5687464904907446607)
XLA Ops:
  0.6 0.7 copy.47
  1.5 0.7 convert_add_fusion
  2.2 1.2 %convert_reduce_fusion = (s32[4,512]{1,0:T(4,128)S(1)}, s32[4,512]{1,0:T(4,128)S(1)}) fusion(s32[4,256]{1,0:T(4,128)S(1)} %convert_add_fusion, s32[4,256]{1,0:T(4,128)} %bitcast.106), kind=kLoop, calls=%fused_computation.28 | loop fusion | flops 2617344 | bytes 24576 | tf_op jit(solution)/shard_map/reduce_sum | solution.py:71
  3.6 0.7 reshape.100
  4.3 8.3 %all-to-all-start = ((s32[16,1,128]{2,1,0:T(1,128)}), s32[16,1,128]{2,1,0:T(1,128)S(1)}, u32[]{:S(2)}, u32[]{:S(2)}) async-start(s32[16,1,128]{2,1,0:T(1,128)} %reshape.100), calls=%async_computation | async-start | bytes 16384 | tf_op jit(solution)/shard_map/all_to_all | solution.py:73
  12.6 7.2 %all-to-all-done = s32[16,1,128]{2,1,0:T(1,128)S(1)} async-done(((s32[16,1,128]{2,1,0:T(1,128)}), s32[16,1,128]{2,1,0:T(1,128)S(1)}, u32[]{:S(2)}, u32[]{:S(2)}) %all-to-all-start) | async-done | bytes 8224 | tf_op jit(solution)/shard_map/all_to_all | solution.py:73
  19.8 0.5 broadcast.66
  20.4 0.7 reduce
  21.3 11.4 %while.30 = (s32[]{:T(128)}, bf16[4,512,128]{2,1,0:T(8,128)(2,1)S(1)}, s32[4,512]{1,0:T(4,128)S(1)}, bf16[4,4096,128]{2,1,0:T(8,128)(2,1)}, s32[]{:T(128)}) while((s32[]{:T(128)}, bf16[4,512,128]{2,1,0:T(8,128)(2,1)S(1)}, s32[4,512]{1,0:T(4,128)S(1)}, bf16[4,4096,128]{2,1,0:T(8,128)(2,1)}, s32[]{:T(128)}) %tuple.54), condition=%wide.region_4.5_spmd, body=%wide.region_3.4_spmd.sunk | while | flops 539033600 | bytes 1186881 | solution.py:80
  21.3 2.8 %fusion.50 = bf16[4,512,128]{2,1,0:T(8,128)(2,1)S(1)} fusion(bf16[4,512,128]{2,1,0:T(8,128)(2,1)S(1)} %get-tuple-element.197, s32[]{:T(128)} %get-tuple-element.196, s32[512]{0:T(512)S(1)} %bitcast.97, bf16[4,4096,128]{2,1,0:T(8,128)(2,1)} %get-tuple-element.204), kind=kOutput, calls=%fused_computation.5.clone.1 | convolution fusion | flops 539033600 | bytes 1182720 | tf_op jit(solution)/shard_map/while/body/eval_jaxpr/dot_general | solution.py:38
  24.1 2.8 %fusion.50 = bf16[4,512,128]{2,1,0:T(8,128)(2,1)S(1)} fusion(bf16[4,512,128]{2,1,0:T(8,128)(2,1)S(1)} %get-tuple-element.197, s32[]{:T(128)} %get-tuple-element.196, s32[512]{0:T(512)S(1)} %bitcast.97, bf16[4,4096,128]{2,1,0:T(8,128)(2,1)} %get-tuple-element.204), kind=kOutput, calls=%fused_computation.5.clone.1 | convolution fusion | flops 539033600 | bytes 1182720 | tf_op jit(solution)/shard_map/while/body/eval_jaxpr/dot_general | solution.py:38
  27.0 2.8 %fusion.50 = bf16[4,512,128]{2,1,0:T(8,128)(2,1)S(1)} fusion(bf16[4,512,128]{2,1,0:T(8,128)(2,1)S(1)} %get-tuple-element.197, s32[]{:T(128)} %get-tuple-element.196, s32[512]{0:T(512)S(1)} %bitcast.97, bf16[4,4096,128]{2,1,0:T(8,128)(2,1)} %get-tuple-element.204), kind=kOutput, calls=%fused_computation.5.clone.1 | convolution fusion | flops 539033600 | bytes 1182720 | tf_op jit(solution)/shard_map/while/body/eval_jaxpr/dot_general | solution.py:38
  29.8 2.8 %fusion.50 = bf16[4,512,128]{2,1,0:T(8,128)(2,1)S(1)} fusion(bf16[4,512,128]{2,1,0:T(8,128)(2,1)S(1)} %get-tuple-element.197, s32[]{:T(128)} %get-tuple-element.196, s32[512]{0:T(512)S(1)} %bitcast.97, bf16[4,4096,128]{2,1,0:T(8,128)(2,1)} %get-tuple-element.204), kind=kOutput, calls=%fused_computation.5.clone.1 | convolution fusion | flops 539033600 | bytes 1182720 | tf_op jit(solution)/shard_map/while/body/eval_jaxpr/dot_general | solution.py:38
  32.6 0.9 copy.32
  33.5 3.6 %all-to-all-start.1 = ((bf16[4,16,32,128]{3,2,0,1:T(8,128)(2,1)}), bf16[4,16,32,128]{3,2,0,1:T(8,128)(2,1)S(1)}, u32[]{:S(2)}, u32[]{:S(2)}) async-start(bf16[4,16,32,128]{3,2,0,1:T(8,128)(2,1)} %copy.32), calls=%async_computation.1 | async-start | bytes 1048576 | tf_op jit(solution)/shard_map/all_to_all | solution.py:86
  37.1 13.9 %all-to-all-done.1 = bf16[4,16,32,128]{3,2,0,1:T(8,128)(2,1)S(1)} async-done(((bf16[4,16,32,128]{3,2,0,1:T(8,128)(2,1)}), bf16[4,16,32,128]{3,2,0,1:T(8,128)(2,1)S(1)}, u32[]{:S(2)}, u32[]{:S(2)}) %all-to-all-start.1) | async-done | bytes 524320 | tf_op jit(solution)/shard_map/all_to_all | solution.py:86
  51.1 1.8 %while.31 = (s32[]{:T(128)}, bf16[4,256,128]{1,2,0:T(8,128)(2,1)S(1)}, s32[4,256]{1,0:T(4,128)S(1)}, bf16[4,512,128]{2,1,0:T(8,128)(2,1)S(1)}, s32[]{:T(128)}) while((s32[]{:T(128)}, bf16[4,256,128]{1,2,0:T(8,128)(2,1)S(1)}, s32[4,256]{1,0:T(4,128)S(1)}, bf16[4,512,128]{2,1,0:T(8,128)(2,1)S(1)}, s32[]{:T(128)}) %tuple.65), condition=%wide.region_6.7_spmd, body=%wide.region_5.6_spmd.sunk | while | flops 33718272 | bytes 461897 | solution.py:89
  53.3 0.6 fusion.32
  54.4 0.6 multiply_reduce_fusion
  55.0 0.5 fusion.27
  55.8 0.6 log_reduce_fusion
  56.8 0.5 fusion.30
  58.8 1.5 %copy.36 = f32[512,640]{1,0:T(8,128)} copy(f32[512,640]{0,1:T(8,128)S(1)} %pad_maximum_fusion) | data formatting | bytes 2621440 | tf_op jit(solution)/shard_map/concatenate | solution.py:356
  60.4 1.9 %while.32 = (s32[]{:T(128)}, bf16[4,512,128]{2,1,0:T(8,128)(2,1)S(1)}, s32[4,256]{1,0:T(4,128)S(1)}, bf16[4,256,128]{2,1,0:T(8,128)(2,1)S(1)}, s32[]{:T(128)}) while((s32[]{:T(128)}, bf16[4,512,128]{2,1,0:T(8,128)(2,1)S(1)}, s32[4,256]{1,0:T(4,128)S(1)}, bf16[4,256,128]{2,1,0:T(8,128)(2,1)S(1)}, s32[]{:T(128)}) %tuple.67), condition=%wide.region_14.15_spmd, body=%wide.region_13.14_spmd.sunk | while | flops 33751040 | bytes 200769 | solution.py:107
  60.4 0.4 fusion.54
  60.8 0.4 fusion.54
  61.3 0.4 fusion.54
  62.2 43.0 %shard_map.128 = (f32[4,2048,128]{2,1,0:T(8,128)}, f32[512,512]{1,0:T(8,128)}, f32[128,512]{1,0:T(8,128)}) custom-call(bf16[4,16,32,128]{3,2,1,0:T(8,128)(2,1)S(1)} %bitcast.89, s32[4,512]{1,0:T(4,128)S(1)} %get-tuple-element.247, f32[2,4,4,16,640]{4,3,2,1,0:T(8,128)} %bitcast.88), custom_call_target="tpu_custom_call" | custom-call | tf_op jit(solution)/shard_map/pallas_call | solution.py:366
  105.2 1.4 %fusion.38 = (f32[1,512]{1,0:T(1,128)}, f32[1,512]{1,0:T(1,128)}) fusion(f32[128,512]{1,0:T(8,128)} %get-tuple-element.79), kind=kLoop, calls=%fused_computation.75 | loop fusion | bytes 8192 | tf_op jit(solution)/shard_map/slice | solution.py:393
  106.6 1.2 %slice.11 = f32[1,1]{1,0:T(1,128)} slice(f32[128,512]{1,0:T(8,128)} %get-tuple-element.79), slice={[2:3], [0:1]} | slice | bytes 8 | tf_op jit(solution)/shard_map/slice | solution.py:393
  107.7 4.6 %copy.76 = f32[4,2048,128]{2,1,0:T(8,128)} copy(f32[4,2048,128]{2,1,0:T(8,128)} %get-tuple-element.241) | data formatting | bytes 8388608
  112.3 1.0 copy.77
  (66 shorter events, 4.6 us)
Async XLA Ops:
  4.3 15.6 %all-to-all-start = ((s32[16,1,128]{2,1,0:T(1,128)}), s32[16,1,128]{2,1,0:T(1,128)S(1)}, u32[]{:S(2)}, u32[]{:S(2)}) async-start(s32[16,1,128]{2,1,0:T(1,128)} %reshape.100), calls=%async_computation | async-start | bytes 16384 | tf_op jit(solution)/shard_map/all_to_all | solution.py:73
  33.5 17.6 %all-to-all-start.1 = ((bf16[4,16,32,128]{3,2,0,1:T(8,128)(2,1)}), bf16[4,16,32,128]{3,2,0,1:T(8,128)(2,1)S(1)}, u32[]{:S(2)}, u32[]{:S(2)}) async-start(bf16[4,16,32,128]{3,2,0,1:T(8,128)(2,1)} %copy.32), calls=%async_computation.1 | async-start | bytes 1048576 | tf_op jit(solution)/shard_map/all_to_all | solution.py:86
  37.1 15.9 %copy-start = (f32[512,512]{1,0:T(8,128)S(1)}, f32[512,512]{1,0:T(8,128)}, u32[]{:S(2)}) copy-start(f32[512,512]{1,0:T(8,128)} %param.21) | copy-start | bytes 3145732
  37.1 15.9 %copy-start.5 = (f32[512]{0:T(512)S(1)}, f32[512]{0:T(512)}, u32[]{:S(2)}) copy-start(f32[512]{0:T(512)} %param.22) | copy-start | bytes 6148
  51.1 2.2 %copy-start.4 = (f32[512]{0:T(512)S(1)}, f32[512]{0:T(512)}, u32[]{:S(2)}) copy-start(f32[512]{0:T(512)} %param.23) | copy-start | bytes 6148
  52.9 1.0 copy-start.6
  52.9 1.0 copy-start.2
  52.9 1.2 %copy-start.3 = (f32[1,256]{1,0:T(1,128)S(1)}, f32[1,256]{1,0:T(1,128)}, u32[]{:S(2)}) copy-start(f32[1,256]{1,0:T(1,128)} %param.19) | copy-start | bytes 3076
  107.7 4.6 %copy-start.1 = (f32[512,512]{1,0:T(8,128)S(1)}, f32[512,512]{1,0:T(8,128)}, u32[]{:S(2)}) copy-start(f32[512,512]{1,0:T(8,128)} %get-tuple-element.242) | copy-start | bytes 3145732

commit v2 on v1

--- a/solution.py
+++ b/solution.py
@@ -70,6 +70,22 @@
     wanted = jnp.sum(slot_hot * rows_now[:, :, None], axis=1) + shard_rows * (
         1 - jnp.sum(slot_hot, axis=1)
     )
+    if (
+        capacity % 16 == 0
+        and table_count * capacity == 128
+        and w_hidden.shape[0] == w_hidden.shape[1]
+    ):
+        return whole_kernel(
+            tables,
+            jnp.transpose(wanted.reshape(table_count, owners, capacity), (1, 0, 2)),
+            slot_of,
+            session_of[0],
+            relevance[0],
+            logit_bias[0],
+            w_hidden,
+            bias_hidden,
+            w_score,
+        )
     requested = lax.all_to_all(
         wanted.reshape(table_count, owners, capacity),
         "table",
@@ -108,16 +124,6 @@
         lambda pair: place_rows(pair[0], pair[1], slot_total).astype(jnp.bfloat16),
         (slot_of, input_grad),
     )
-    if capacity % 16 == 0 and w_hidden.shape[0] == w_hidden.shape[1]:
-        return finish_kernel(
-            outgoing.reshape(table_count, owners, capacity, emb_width),
-            requested.reshape(table_count, slot_total),
-            weight_grad,
-            bias_grad,
-            score_weight_grad,
-            loss_sum,
-            shard_rows,
-        )
     incoming = lax.all_to_all(
         outgoing.reshape(table_count, owners, capacity, emb_width),
         "table",
@@ -152,19 +158,28 @@
 MESH = pl.DeviceIdType.MESH
 
 
-def finish_body(
-    sizes, out_ref, ids_ref, dense_ref, emb_ref, step_ref, small_ref,
-    grads, swapped, ids_other, emb_rows, from_other, from_plane, from_column, sum_pair, sum_plane,
+def whole_body(
+    sizes, tables_hbm, wanted_ref, slots_ref, columns_ref, weights_ref, bias_ref, scorer_ref,
+    emb_ref, step_ref, small_ref,
+    tables_ref, ids_in, ids_ref, served, picked, picked_rows, gathered, dense_ref, out_ref,
+    load_sem, want_sems, want_own, serve_send, serve_recv, serve_own, grads, swapped, ids_other, emb_rows, from_other, from_plane, from_column, sum_pair, sum_plane,
     total, grad_send, grad_recv, own_sem, swap_send, swap_recv, ids_sems, pair_sems, plane_send,
     plane_recv, column_send, column_recv, emb_sem,
 ):
-    tables, owners, capacity, width, half_rows, inner, outer, hid, sessions = sizes
+    tables, owners, capacity, width, half_rows, inner, outer, hid, sessions, own_sessions = sizes
     slots = owners * capacity
     me = lax.axis_index("table")
     core = lax.axis_index("dp")
     low, high = lax.rem(me, inner), me // inner
     other = (me, 1 - core)
 
+    def load(table):
+        return pltpu.make_async_copy(
+            tables_hbm.at[table], tables_ref.at[table], load_sem.at[table]
+        )
+
+    for table in range(tables):
+        load(table).start()
     barrier = pltpu.get_barrier_semaphore()
 
     def greet(step, carry):
@@ -183,10 +198,135 @@
             device_id_type=MESH,
         )
 
+    def to_peers(copy_to):
+        def one(step, carry):
+            copy_to(lax.rem(me + step, owners)).start()
+            return carry
+
+        lax.fori_loop(1, owners, one, 0)
+
+    to_peers(
+        lambda peer: remote(
+            wanted_ref.at[peer], ids_in.at[me], want_sems.at[0], want_sems.at[1], (peer, core)
+        )
+    )
+    want_mine = pltpu.make_async_copy(wanted_ref.at[me], ids_in.at[me], want_own.at[0])
+    want_mine.start()
+    w_bf = weights_ref[...].astype(jnp.bfloat16)
+    want_mine.wait()
+    remote(
+        wanted_ref.at[pl.ds(0, owners - 1)], ids_in.at[pl.ds(0, owners - 1)], want_sems.at[0],
+        want_sems.at[1], other,
+    ).wait()
+
+    depth = 1024
+    shard_rows = 2 * half_rows
+
+    def serve_own_copy(table):
+        return pltpu.make_async_copy(
+            served.at[table, me], picked.at[table, me], serve_own.at[table]
+        )
+
+    for table in range(tables):
+        named = jnp.broadcast_to(
+            ids_in[:, 0:1, :].astype(jnp.float32), (owners, capacity, 128)
+        )
+        lane = lax.broadcasted_iota(jnp.int32, named.shape, 2)
+        place_in = lax.broadcasted_iota(jnp.int32, named.shape, 1) + table * capacity
+        wide_ids = jnp.broadcast_to(
+            jnp.sum(jnp.where(lane == place_in, named, 0.0), axis=2, keepdims=True), named.shape
+        ).reshape(slots, 128).astype(jnp.int32)
+        ids_ref[pl.ds(table, 1), :] = wide_ids.T[0:1, :]
+        ids_col = wide_ids[:, 0:1]
+        load(table).wait()
+        picked_rows[...] = jnp.zeros_like(picked_rows)
+
+        def pick_block(step, carry):
+            at = lax.broadcasted_iota(jnp.int32, (slots, depth), 1)
+            hot = jnp.where(at == ids_col - step * depth, 1.0, 0.0).astype(jnp.bfloat16)
+            rows_at = pl.ds(pl.multiple_of(step * depth, depth), depth)
+            picked_rows[...] += jnp.dot(
+                hot, tables_ref[table, rows_at, :], preferred_element_type=jnp.float32
+            )
+            return carry
+
+        lax.fori_loop(0, shard_rows // depth, pick_block, 0)
+        served[table] = picked_rows[...].astype(jnp.bfloat16).reshape(owners, capacity, width)
+        serve_own_copy(table).start()
+        to_peers(
+            lambda peer, table=table: remote(
+                served.at[table, peer], picked.at[table, me], serve_send.at[table],
+                serve_recv.at[table], (peer, core),
+            )
+        )
+    ids_copy = remote(ids_ref, ids_other, ids_sems.at[0], ids_sems.at[1], other)
+    ids_copy.start()
+
+    imps = gathered.shape[0]
+    for table in range(tables):
+        serve_own_copy(table).wait()
+        remote(
+            served.at[table, pl.ds(0, owners - 1)], picked.at[table, pl.ds(0, owners - 1)],
+            serve_send.at[table], serve_recv.at[table], other,
+        ).wait()
+        slot_col = columns_ref[:, table : table + 1].astype(jnp.int32)
+        hot = jnp.where(
+            lax.broadcasted_iota(jnp.int32, (imps, slots), 1) == slot_col, 1.0, 0.0
+        ).astype(jnp.bfloat16)
+        gathered[:, table * width : (table + 1) * width] = jnp.dot(
+            hot, picked[table].reshape(slots, width), preferred_element_type=jnp.float32
+        ).astype(jnp.bfloat16)
+    inputs = gathered[...]
+    pre_act = jnp.dot(inputs, w_bf, preferred_element_type=jnp.float32) + bias_ref[...]
+    logistic = 1.0 / (1.0 + jnp.exp(-pre_act))
+    hidden = pre_act * logistic
+    session = columns_ref[:, tables : tables + 1].astype(jnp.int32)
+    relevance = columns_ref[:, tables + 1 : tables + 2]
+    scores = jnp.sum(hidden * scorer_ref[...], axis=1, keepdims=True)
+    scores = scores + columns_ref[:, tables + 2 : tables + 3]
+    member = lax.broadcasted_iota(jnp.int32, (imps, 128), 1) == session
+    highest = jnp.max(jnp.where(member, scores, -jnp.inf), axis=0, keepdims=True)
+    highest_each = jnp.sum(jnp.where(member, highest, 0.0), axis=1, keepdims=True)
+    shifted = scores - highest_each
+    exponent = jnp.exp(shifted)
+    totals = jnp.sum(jnp.where(member, exponent, 0.0), axis=0, keepdims=True)
+    weights = jnp.sum(jnp.where(member, relevance, 0.0), axis=0, keepdims=True)
+    total_each = jnp.sum(jnp.where(member, totals, 0.0), axis=1, keepdims=True)
+    weight_each = jnp.sum(jnp.where(member, weights, 0.0), axis=1, keepdims=True)
+    target = relevance / weight_each
+    real = lax.broadcasted_iota(jnp.int32, (1, 128), 1) < own_sessions
+    loss_sum = jnp.sum(jnp.log(jnp.where(real, totals, 1.0)), keepdims=True) - jnp.sum(
+        target * shifted, keepdims=True
+    )
+    score_grad = exponent / total_each - target
+    pre_grad = score_grad * scorer_ref[...] * (logistic * (1.0 + pre_act * (1.0 - logistic)))
+    pre_grad_bf = pre_grad.astype(jnp.bfloat16)
+    weight_grad = lax.dot_general(
+        inputs, pre_grad_bf, (((0,), (0,)), ((), ())), preferred_element_type=jnp.float32
+    )
+    bias_grad = jnp.sum(pre_grad, axis=0, keepdims=True)
+    score_weight_grad = jnp.sum(score_grad * hidden, axis=0, keepdims=True)
+    line = lax.broadcasted_iota(jnp.int32, (128, hid), 0)
+    spot = lax.broadcasted_iota(jnp.int32, (128, hid), 1)
+    extra = jnp.where(line == 0, bias_grad, 0.0) + jnp.where(line == 1, score_weight_grad, 0.0)
+    extra = extra + jnp.where((line == 2) & (spot == 0), loss_sum, 0.0)
+    dense_ref[:, :, :, :, :hid] = weight_grad.reshape(dense_ref.shape[:4] + (hid,))
+    dense_ref[:, :, :, :, hid:] = extra.T.reshape(dense_ref.shape[:4] + (128,))
     pair_up = remote(dense_ref.at[1 - core], from_other, pair_sems.at[0], pair_sems.at[1], other)
     pair_up.start()
-    ids_copy = remote(ids_ref, ids_other, ids_sems.at[0], ids_sems.at[1], other)
-    ids_copy.start()
+    input_grad = lax.dot_general(
+        pre_grad_bf, w_bf, (((1,), (1,)), ((), ())), preferred_element_type=jnp.float32
+    ).astype(jnp.bfloat16)
+
+    def fill(table):
+        hot = jnp.where(
+            lax.broadcasted_iota(jnp.int32, (slots, imps), 0) == slots_ref[pl.ds(table, 1), :],
+            1.0, 0.0,
+        ).astype(jnp.bfloat16)
+        out_ref[table] = jnp.dot(
+            hot, input_grad[:, table * width : (table + 1) * width],
+            preferred_element_type=jnp.float32,
+        ).astype(jnp.bfloat16).reshape(owners, capacity, width)
 
     def own_copy(table):
         return pltpu.make_async_copy(
@@ -194,6 +334,7 @@
         )
 
     def send_grads(table):
+        fill(table)
         own_copy(table).start()
 
         def send_one(step, carry):
@@ -332,64 +473,77 @@
         emb_copy(table).wait()
 
 
-def finish_kernel(outgoing, requested, weight_grad, bias_grad, score_grad, loss_sum, shard_rows):
-    tables, owners, capacity, width = outgoing.shape
-    hid = weight_grad.shape[0]
+def whole_kernel(
+    tables, wanted, slot_of, session, relevance, logit_bias, w_hidden, bias_hidden, w_score
+):
+    table_count, shard_rows, width = tables.shape
+    owners, _, capacity = wanted.shape
+    hid = w_hidden.shape[1]
+    imps = session.shape[0]
+    slots = owners * capacity
     half_rows = shard_rows // 2
     inner = 1
     while inner * inner < owners:
         inner *= 2
     outer = owners // inner
     rows = hid // (2 * owners)
-    lane = jnp.arange(128, dtype=jnp.int32)[None, :]
-    extra = jnp.where(
-        lane == 0,
-        bias_grad[:, None],
-        jnp.where(
-            lane == 1,
-            score_grad[:, None],
-            jnp.where(
-                (lane == 2) & (jnp.arange(hid, dtype=jnp.int32)[:, None] == 0), loss_sum, 0.0
-            ),
-        ),
-    )
-    dense = jnp.concatenate([weight_grad, extra], axis=1)
-    wide = dense.shape[1]
-    dense = dense.reshape(2, inner, outer, rows, wide)
+    wide = hid + 128
+    wanted = jnp.broadcast_to(
+        wanted.reshape(owners, 1, table_count * capacity), (owners, 8, table_count * capacity)
+    )
+    columns = jnp.stack(
+        [slot_of[table].astype(jnp.float32) for table in range(table_count)]
+        + [session.astype(jnp.float32), relevance, logit_bias],
+        axis=1,
+    )
     sizes = (
-        tables, owners, capacity, width, half_rows, inner, outer, hid,
-        SESS_DEV * owners * 2,
+        table_count, owners, capacity, width, half_rows, inner, outer, hid,
+        SESS_DEV * owners * 2, SESS_DEV,
     )
     f32, bf16 = jnp.float32, jnp.bfloat16
     dma = pltpu.SemaphoreType.DMA
     vmem = pl.BlockSpec(memory_space=pltpu.VMEM)
     emb_step, step_hidden, small = pl.pallas_call(
-        functools.partial(finish_body, sizes),
+        functools.partial(whole_body, sizes),
         out_shape=(
-            jax.ShapeDtypeStruct((tables, half_rows, width), f32),
+            jax.ShapeDtypeStruct((table_count, half_rows, width), f32),
             jax.ShapeDtypeStruct((hid, hid), f32),
             jax.ShapeDtypeStruct((128, hid), f32),
         ),
-        in_specs=[vmem] * 3,
+        in_specs=[pl.BlockSpec(memory_space=pl.ANY)] + [vmem] * 6,
         out_specs=(pl.BlockSpec(memory_space=pl.ANY), vmem, vmem),
         scratch_shapes=[
-            pltpu.VMEM((tables, owners, capacity, width), bf16),
-            pltpu.VMEM((tables, owners, capacity, width), bf16),
-            pltpu.VMEM(requested.shape, jnp.int32),
-            pltpu.VMEM((tables, half_rows, width), f32),
+            pltpu.VMEM(tables.shape, bf16),
+            pltpu.VMEM(wanted.shape, jnp.int32),
+            pltpu.VMEM((table_count, slots), jnp.int32),
+            pltpu.VMEM((table_count, owners, capacity, width), bf16),
+            pltpu.VMEM((table_count, owners, capacity, width), bf16),
+            pltpu.VMEM((slots, width), f32),
+            pltpu.VMEM((imps, table_count * width), bf16),
+            pltpu.VMEM((2, inner, outer, rows, wide), f32),
+            pltpu.VMEM((table_count, owners, capacity, width), bf16),
+            dma((table_count,)), dma((2,)), dma((1,)),
+            dma((table_count,)), dma((table_count,)), dma((table_count,)),
+            pltpu.VMEM((table_count, owners, capacity, width), bf16),
+            pltpu.VMEM((table_count, owners, capacity, width), bf16),
+            pltpu.VMEM((table_count, slots), jnp.int32),
+            pltpu.VMEM((table_count, half_rows, width), f32),
             pltpu.VMEM((inner, outer, rows, wide), f32),
             pltpu.VMEM((inner - 1, outer, rows, wide), f32),
             pltpu.VMEM((outer - 1, rows, wide), f32),
             pltpu.VMEM((inner, outer, rows, wide), f32),
             pltpu.VMEM((outer, rows, wide), f32),
             pltpu.VMEM((2, inner, outer, rows, wide), f32),
-            dma((tables,)), dma((tables,)), dma((tables,)), dma((tables,)), dma((tables,)),
+            dma((table_count,)), dma((table_count,)), dma((table_count,)),
+            dma((table_count,)), dma((table_count,)),
             dma((2,)), dma((4,)),
             dma((2, inner - 1)), dma((2, inner - 1)), dma((2, outer - 1)), dma((2, outer - 1)),
-            dma((tables,)),
+            dma((table_count,)),
         ],
-        compiler_params=pltpu.CompilerParams(collective_id=1, has_side_effects=True),
-    )(outgoing, requested, dense)
+        compiler_params=pltpu.CompilerParams(
+            collective_id=1, has_side_effects=True, vmem_limit_bytes=60 * 1024 * 1024
+        ),
+    )(tables, wanted, slot_of, columns, w_hidden, bias_hidden[None, :], w_score[None, :])
     return (emb_step, step_hidden, small[0], small[1], small[2, 0])
 
 

time: 114 us -> 83.7 us (0.73)
  Pallas kernels: 43 us -> 68.6 us
  waiting for transfers between devices: 21.1 us -> 0 us
  matrix products: 16.5 us -> 0.21 us
  starting transfers between devices: 11.9 us -> 0 us
  local copies, waits for them, and re-layouts: 13.4 us -> 11.1 us
  other arithmetic: 4.77 us -> 2.61 us
  between operations: 2.21 us -> 0.67 us
    pallas_call x1, Pallas kernels: 43 us -> 68.6 us  [whole_kernel(): pl.pallas_call(functools.partial(whole_body, sizes), out_shape=(jax.Shape...]
    all_to_all x2 -> x0, waiting for transfers between devices: 21.1 us -> none  [the longest x1 13.9 us: on_device(): lax.all_to_all(served, 'table', split_axis=1, concat_axis=1, tiled=True)]
    dot_general x17 -> x0, matrix products: 16.3 us -> none  [the longest x8 12.3 us: pick_rows(): jnp.dot(selector(indices, source.shape[0]), source, preferred_element_typ...]
    all_to_all x2 -> x0, starting transfers between devices: 11.9 us -> none  [the longest x1 8.34 us: on_device(): lax.all_to_all(wanted.reshape(table_count, owners, capacity), 'table', sp...]
    reduce_sum x6 -> x0, other arithmetic: 1.79 us -> none  [the longest x2 1.22 us: session_terms(): loss_sum = jnp.sum(jnp.log(totals)) - jnp.sum(target * shifted)]
    concatenate x1 -> x0, local copies, waits for them, and re-layouts: 1.46 us -> none  [finish_kernel(): dense = jnp.concatenate([weight_grad, extra], axis=1)]
    another operation x2, local copies, waits for them, and re-layouts: 0.14 us -> 1.52 us  [whole_kernel(): jnp.stack([slot_of[table].astype(jnp.float32) for table in range(table_co...]
    unnamed x19 -> x7, local copies, waits for them, and re-layouts: 7.04 us -> 6.23 us
  transfers between devices with their start and end apart: 2 -> 0, of which waited for: 2 -> 0; matrix products, arithmetic and copies ran while one was open for 0% -> 0% of each run, Pallas kernels for 0% -> 0%
where the time goes in v2:
time: 83.7 us; the launch traced here: 83.3 us
  Pallas kernels  68.6 us (82%)
  local copies, waits for them, and re-layouts  11.1 us (13%)
  other arithmetic  2.61 us (3%)
    pallas_call x1, Pallas kernels, whole_kernel(): pl.pallas_call(functools.partial(whole_body, sizes), out_shape=(jax.Shape...  68.6 us
    unnamed x7, local copies, waits for them, and re-layouts  6.23 us
    slice x2, local copies, waits for them, and re-layouts, whole_kernel(): return (emb_step, step_hidden, small[0], small[1], small[2, 0])  2.57 us

profile of v2, /device:TPU:0, one launch (start us, length us, event | category | flops | bytes accessed | tf_op | source)
XLA Modules:
  0.0 83.3 jit_solution(14216531886805906718)
XLA Ops:
  0.6 0.7 copy.37
  1.3 0.2 fusion.1
  1.5 0.7 convert_add_fusion.slots_ref
  2.2 0.0 copy-start.1
  2.2 0.7 fusion.5
  2.9 0.7 stack.2
  3.6 0.8 copy.32.columns_ref
  4.4 1.2 %convert_reduce_fusion = (s32[4,512]{1,0:T(4,128)S(1)}, s32[4,512]{1,0:T(4,128)S(1)}) fusion(s32[4,256]{1,0:T(4,128)S(1)} %convert_add_fusion.slots_ref, s32[4,256]{1,0:T(4,128)} %bitcast.35), kind=kLoop, calls=%fused_computation | loop fusion | flops 2617344 | bytes 24576 | tf_op jit(solution)/shard_map/reduce_sum | solution.py:71
  5.7 0.1 add.17
  5.8 0.1 broadcast_in_dim.8
  5.9 0.6 broadcast_in_dim.9.wanted_ref
  6.5 0.0 copy-done.1
  6.5 68.6 %shard_map.128 = (f32[4,2048,128]{2,1,0:T(8,128)}, f32[512,512]{1,0:T(8,128)}, f32[128,512]{1,0:T(8,128)}) custom-call(bf16[4,4096,128]{2,1,0:T(8,128)(2,1)} %tables_hbm.1, s32[16,8,128]{2,1,0:T(8,128)} %broadcast_in_dim.9.wanted_ref, s32[4,256]{1,0:T(4,128)} %copy-done.1, f32[256,7]{1,0:T(8,128)} %copy.32.columns_ref, f32[512,512]{1,0:T(8,128)} %weights_ref.1, ...), custom_call_target="tpu_custom_call" | custom-call | tf_op jit(solution)/shard_map/pallas_call | solution.py:506
  75.1 1.4 %fusion.9 = (f32[1,512]{1,0:T(1,128)}, f32[1,512]{1,0:T(1,128)}) fusion(f32[128,512]{1,0:T(8,128)} %get-tuple-element.10), kind=kLoop, calls=%fused_computation.22 | loop fusion | bytes 8192 | tf_op jit(solution)/shard_map/slice | solution.py:547
  76.5 1.2 %slice.27 = f32[1,1]{1,0:T(1,128)} slice(f32[128,512]{1,0:T(8,128)} %get-tuple-element.10), slice={[2:3], [0:1]} | slice | bytes 8 | tf_op jit(solution)/shard_map/slice | solution.py:547
  77.7 0.0 copy-start
  77.7 4.6 %copy.40 = f32[4,2048,128]{2,1,0:T(8,128)} copy(f32[4,2048,128]{2,1,0:T(8,128)} %get-tuple-element.25) | data formatting | bytes 8388608
  82.3 0.0 copy-done
  82.3 1.0 %copy.41 = f32[512,512]{1,0:T(8,128)} copy(f32[512,512]{1,0:T(8,128)S(1)} %copy-done) | data formatting | bytes 2097152
  (2 shorter events, 0.0 us)
Async XLA Ops:
  2.2 4.3 %copy-start.1 = (s32[4,256]{1,0:T(4,128)}, s32[4,256]{1,0:T(4,128)S(1)}, u32[]{:S(2)}) copy-start(s32[4,256]{1,0:T(4,128)S(1)} %convert_add_fusion.slots_ref) | copy-start | bytes 12292
  77.7 4.6 %copy-start = (f32[512,512]{1,0:T(8,128)S(1)}, f32[512,512]{1,0:T(8,128)}, u32[]{:S(2)}) copy-start(f32[512,512]{1,0:T(8,128)} %get-tuple-element.26) | copy-start | bytes 3145732

commit v3 on v2

--- a/solution.py
+++ b/solution.py
@@ -423,8 +423,7 @@
     sum_pair[...] = dense_ref[core] + from_other[...]
     plane_sum = plane_copies(0, lambda to: sum_pair.at[to], lambda slot: from_plane.at[slot])
     run(plane_sum)
-    for table in range(1, tables):
-        send_grads(table)
+    send_grads(1)
     ids_copy.wait()
     finish(plane_sum)
     part = sum_pair[low]
@@ -433,6 +432,7 @@
     sum_plane[...] = part
     column_sum = column_copies(0, lambda to: sum_plane.at[to], lambda slot: from_column.at[slot])
     run(column_sum)
+    send_grads(2)
     arrive(0)
     finish(column_sum)
     part = sum_plane[high]
@@ -443,17 +443,27 @@
         1, lambda to: total.at[core, low, high], lambda slot: total.at[core, low, high]
     )
     run(column_share)
+
+    def plane_share(step):
+        source = lax.rem(high + outer - step, outer)
+        return plane_copies(
+            1 + step,
+            lambda to: total.at[core, low, source],
+            lambda slot: total.at[core, low, source],
+        )
+
+    run(plane_share(0))
+    for table in range(3, tables):
+        send_grads(table)
     place(0)
+    for step in range(1, outer):
+        column_share[step - 1].wait()
+        run(plane_share(step))
     for table in range(1, tables):
-        if table == 1:
-            finish(column_share)
-            plane_share = plane_copies(
-                1, lambda to: total.at[core, low], lambda slot: total.at[core, low]
-            )
-            run(plane_share)
         arrive(table)
         if table == tables - 1:
-            finish(plane_share)
+            for step in range(outer):
+                finish(plane_share(step))
             pair_down = remote(
                 total.at[core], total.at[core], pair_sems.at[2], pair_sems.at[3], other
             )
@@ -537,7 +547,7 @@
             dma((table_count,)), dma((table_count,)), dma((table_count,)),
             dma((table_count,)), dma((table_count,)),
             dma((2,)), dma((4,)),
-            dma((2, inner - 1)), dma((2, inner - 1)), dma((2, outer - 1)), dma((2, outer - 1)),
+            dma((1 + outer, inner - 1)), dma((1 + outer, inner - 1)), dma((2, outer - 1)), dma((2, outer - 1)),
             dma((table_count,)),
         ],
         compiler_params=pltpu.CompilerParams(

time: 83.7 us -> 84.8 us (1.013)
  Pallas kernels: 68.6 us -> 69.7 us
    pallas_call x1, Pallas kernels: 68.6 us -> 69.7 us  [whole_kernel(): pl.pallas_call(functools.partial(whole_body, sizes), out_shape=(jax.Shape...]
where the time goes in v3:
time: 84.8 us; the launch traced here: 84.4 us
  Pallas kernels  69.7 us (82%)
  local copies, waits for them, and re-layouts  11.1 us (13%)
  other arithmetic  2.61 us (3%)
    pallas_call x1, Pallas kernels, whole_kernel(): pl.pallas_call(functools.partial(whole_body, sizes), out_shape=(jax.Shape...  69.7 us
    unnamed x7, local copies, waits for them, and re-layouts  6.23 us
    slice x2, local copies, waits for them, and re-layouts, whole_kernel(): return (emb_step, step_hidden, small[0], small[1], small[2, 0])  2.57 us

profile of v3, /device:TPU:0, one launch (start us, length us, event | category | flops | bytes accessed | tf_op | source)
XLA Modules:
  0.0 84.4 jit_solution(7580062100382449035)
XLA Ops:
  0.6 0.7 copy.37
  1.3 0.2 fusion.1
  1.5 0.7 convert_add_fusion.slots_ref
  2.2 0.0 copy-start.1
  2.2 0.7 fusion.5
  2.9 0.7 stack.2
  3.6 0.8 copy.32.columns_ref
  4.4 1.2 %convert_reduce_fusion = (s32[4,512]{1,0:T(4,128)S(1)}, s32[4,512]{1,0:T(4,128)S(1)}) fusion(s32[4,256]{1,0:T(4,128)S(1)} %convert_add_fusion.slots_ref, s32[4,256]{1,0:T(4,128)} %bitcast.35), kind=kLoop, calls=%fused_computation | loop fusion | flops 2617344 | bytes 24576 | tf_op jit(solution)/shard_map/reduce_sum | solution.py:71
  5.7 0.1 add.17
  5.8 0.1 broadcast_in_dim.8
  5.9 0.6 broadcast_in_dim.9.wanted_ref
  6.5 0.0 copy-done.1
  6.5 69.7 %shard_map.128 = (f32[4,2048,128]{2,1,0:T(8,128)}, f32[512,512]{1,0:T(8,128)}, f32[128,512]{1,0:T(8,128)}) custom-call(bf16[4,4096,128]{2,1,0:T(8,128)(2,1)} %tables_hbm.1, s32[16,8,128]{2,1,0:T(8,128)} %broadcast_in_dim.9.wanted_ref, s32[4,256]{1,0:T(4,128)} %copy-done.1, f32[256,7]{1,0:T(8,128)} %copy.32.columns_ref, f32[512,512]{1,0:T(8,128)} %weights_ref.1, ...), custom_call_target="tpu_custom_call" | custom-call | tf_op jit(solution)/shard_map/pallas_call | solution.py:516
  76.3 1.4 %fusion.9 = (f32[1,512]{1,0:T(1,128)}, f32[1,512]{1,0:T(1,128)}) fusion(f32[128,512]{1,0:T(8,128)} %get-tuple-element.10), kind=kLoop, calls=%fused_computation.22 | loop fusion | bytes 8192 | tf_op jit(solution)/shard_map/slice | solution.py:557
  77.6 1.2 %slice.27 = f32[1,1]{1,0:T(1,128)} slice(f32[128,512]{1,0:T(8,128)} %get-tuple-element.10), slice={[2:3], [0:1]} | slice | bytes 8 | tf_op jit(solution)/shard_map/slice | solution.py:557
  78.8 0.0 copy-start
  78.8 4.6 %copy.40 = f32[4,2048,128]{2,1,0:T(8,128)} copy(f32[4,2048,128]{2,1,0:T(8,128)} %get-tuple-element.25) | data formatting | bytes 8388608
  83.4 0.0 copy-done
  83.4 1.0 %copy.41 = f32[512,512]{1,0:T(8,128)} copy(f32[512,512]{1,0:T(8,128)S(1)} %copy-done) | data formatting | bytes 2097152
  (2 shorter events, 0.0 us)
Async XLA Ops:
  2.2 4.3 %copy-start.1 = (s32[4,256]{1,0:T(4,128)}, s32[4,256]{1,0:T(4,128)S(1)}, u32[]{:S(2)}) copy-start(s32[4,256]{1,0:T(4,128)S(1)} %convert_add_fusion.slots_ref) | copy-start | bytes 12292
  78.8 4.6 %copy-start = (f32[512,512]{1,0:T(8,128)S(1)}, f32[512,512]{1,0:T(8,128)}, u32[]{:S(2)}) copy-start(f32[512,512]{1,0:T(8,128)} %get-tuple-element.26) | copy-start | bytes 3145732
